TPU v7x, 32 devices: a whole 2x2x4 slice. The times are simulated.
32 devices in a mesh: vtx: 8 (over z, x), src: 4 (over y, core).
Axes of the slice: x: 2, y: 2, z: 4, core: 2. Of those that a mesh axis runs over, the one named last changes fastest.
Arguments:
- heat: float32 [64, 64, 8192], P(None, ('vtx', 'src')), may hold values from -12 to 12
- cotan: float32 [4, 64, 8192], P(None, 'vtx'), may hold values from 0.2 to 2
- source_index: int32 [64], replicated, may hold values from 0 to 524287
Outputs:
- normalised: float32 [64, 64, 8192], P('src', 'vtx')
- col_norm: float32 [64], P('src')
Inputs may be any that keep to these rules, and one draw needn't show every extreme that they name: `source_index`: row-major vertex indices, sources may share a vertex.
All inputs are finite; a program needn't handle non-finite values.
Results may differ from a plain program's by a relative error of at most 0.0003.
Values sent between devices are 32-bit elements; how exact they have to be, the bound alone decides.
A program may use at most 64 MiB of HBM per device.

v0:
```python
import math
import jax
import jax.numpy as jnp
from jax import lax
from jax.sharding import PartitionSpec as P


def from_behind(value, axis, by):
    peers = lax.axis_size(axis)
    pairs = [(i, i + by) for i in range(peers) if 0 <= i + by < peers]
    return lax.ppermute(value, axis, pairs)


def extended(value, sides, width):
    for axis, dim in sides:
        peers, length = (lax.axis_size(axis), value.shape[dim])
        up = [(i, (i + 1) % peers) for i in range(peers - 1)]
        down = [(j, i) for i, j in up]
        last = lax.slice_in_dim(value, length - width, length, axis=dim)
        first = lax.slice_in_dim(value, 0, width, axis=dim)
        before = lax.ppermute(last, axis, up)
        after = lax.ppermute(first, axis, down)
        value = jnp.concatenate([before, value, after], axis=dim)
    return value


def from_right(values):
    return jnp.concatenate([values[..., 1:], jnp.zeros_like(values[..., :1])], axis=-1)


def from_left(values):
    return jnp.concatenate([jnp.zeros_like(values[..., :1]), values[..., :-1]], axis=-1)


def masked_cotan(cotan, row_start, total_rows):
    shape = cotan.shape[1:]
    rows = row_start + lax.broadcasted_iota(jnp.int32, shape, 0)
    cols = lax.broadcasted_iota(jnp.int32, shape, 1)
    inside_col = cols < shape[1] - 1
    inside_row = rows < total_rows - 1
    mass = cotan[0]
    east = jnp.where(inside_col, cotan[1], 0.0)
    north = jnp.where(inside_row, cotan[2], 0.0)
    diag = jnp.where(inside_col & inside_row, cotan[3], 0.0)
    return (mass, east, north, diag)


def stencil_defect(padded, mass, east, north_ext, diag_ext, row_start, sources, amplitude):
    center = padded[:, 1:-1, :]
    above = padded[:, 2:, :]
    below = padded[:, :-2, :]
    north = north_ext[1:]
    south_weight = north_ext[:-1]
    diag = diag_ext[1:]
    southwest_weight = from_left(diag_ext[:-1])
    west_weight = from_left(east)
    result = mass * center + east * (center - from_right(center))
    result = result + west_weight * (center - from_left(center))
    result = result + north * (center - above) + south_weight * (center - below)
    result = (
        result
        + diag * (center - from_right(above))
        + southwest_weight * (center - from_left(below))
    )
    count_rows, width = (center.shape[1], center.shape[2])
    row_ids = row_start + lax.broadcasted_iota(jnp.int32, (count_rows, width), 0)
    col_ids = lax.broadcasted_iota(jnp.int32, (count_rows, width), 1)
    flat = row_ids * width + col_ids
    delta = (flat[None, :, :] == sources[:, None, None]).astype(jnp.float32)
    return result - amplitude * delta


def on_device(heat, cotan, source_index):
    vtx_index = lax.axis_index("vtx")
    rows_dev = cotan.shape[1]
    width = cotan.shape[2]
    total_rows = rows_dev * lax.axis_size("vtx")
    amplitude = math.sqrt(total_rows * width) / 8.0
    block_start = vtx_index * rows_dev
    mass, east, north, diag = masked_cotan(cotan, block_start, total_rows)
    lower = from_behind(jnp.stack([north[-1:], diag[-1:]]), "vtx", 1)
    north_ext = jnp.concatenate([lower[0], north], axis=0)
    diag_ext = jnp.concatenate([lower[1], diag], axis=0)
    src_index = lax.axis_index("src")
    per_group = heat.shape[0] // lax.axis_size("src")
    tile = lax.all_to_all(heat, "src", split_axis=0, concat_axis=1, tiled=True)
    padded = extended(tile, (("vtx", 1),), 1)
    sources = lax.dynamic_slice_in_dim(source_index, src_index * per_group, per_group)
    defect = stencil_defect(
        padded, mass, east, north_ext, diag_ext, block_start, sources, amplitude
    )
    total = lax.psum(jnp.sum(defect * defect, axis=(1, 2)), "vtx")
    norms = jnp.sqrt(total / (total_rows * width) + 1e-06)
    return (defect / norms[:, None, None], norms)


def solution(mesh):
    return jax.shard_map(
        on_device,
        mesh=mesh,
        in_specs=(P(None, ("vtx", "src"), None), P(None, "vtx", None), P()),
        out_specs=(P("src", "vtx", None), P("src")),
        check_vma=False,
    )
```

profile of v0, /device:TPU:0, one launch (start us, length us, event | category | flops | bytes accessed | tf_op | source)
XLA Modules:
  0.0 121.2 jit_solution(14948934049001628183)
XLA Ops:
  0.6 0.0 copy-start
  0.6 5.0 %all-to-all-start = ((f32[64,2,8192]{2,1,0:T(2,128)}), f32[64,2,8192]{2,1,0:T(2,128)}, u32[]{:S(2)}, u32[]{:S(2)}) async-start(f32[64,2,8192]{2,1,0:T(2,128)} %param.3), calls=%async_computation | async-start | bytes 8388608 | tf_op jit(solution)/shard_map/all_to_all | solution.py:86
  5.6 0.0 copy-start.2
  5.7 0.0 copy-done
  5.7 0.1 bitcast_select_fusion.1
  5.9 0.1 pad_maximum_fusion.1
  5.9 4.9 %collective-permute-start.1 = (f32[2,1,8192]{2,1,0:T(1,128)S(1)}, f32[2,1,8192]{2,1,0:T(1,128)S(1)}, u32[]{:S(2)}, u32[]{:S(2)}) collective-permute-start(f32[2,1,8192]{2,1,0:T(1,128)S(1)} %pad_maximum_fusion.1), channel_id=1, source_target_pairs={{0,4},{4,8},{8,12},{12,16},{16,20},{20,24},{24,28},{1,5},{5,9},{9,... | collective-permute-start | bytes 196616 | tf_op jit(solution)/shard_map/ppermute | solution.py:11
  10.8 0.1 slice_bitcast_fusion
  11.0 0.1 iota_add_fusion
  11.1 0.0 copy-done.2
  11.1 0.1 dynamic_slice.3
  11.2 0.1 concatenate.32
  11.3 1.4 %collective-permute-done.1 = f32[2,1,8192]{2,1,0:T(1,128)S(1)} collective-permute-done((f32[2,1,8192]{2,1,0:T(1,128)S(1)}, f32[2,1,8192]{2,1,0:T(1,128)S(1)}, u32[]{:S(2)}, u32[]{:S(2)}) %collective-permute-start.1) | collective-permute-done | bytes 65568 | tf_op jit(solution)/shard_map/ppermute | solution.py:11
  12.8 0.2 select_maximum_fusion.2
  13.0 41.6 %all-to-all-done = f32[64,2,8192]{2,1,0:T(2,128)} async-done(((f32[64,2,8192]{2,1,0:T(2,128)}), f32[64,2,8192]{2,1,0:T(2,128)}, u32[]{:S(2)}, u32[]{:S(2)}) %all-to-all-start) | async-done | bytes 4194336 | tf_op jit(solution)/shard_map/all_to_all | solution.py:86
  54.5 4.6 %copy.6 = f32[4,16,2,8192]{3,1,2,0:T(8,128)S(1)} copy(f32[4,16,2,8192]{3,2,1,0:T(2,128)} %bitcast.1) | data formatting | bytes 8388608 | tf_op jit(solution)/shard_map/all_to_all | solution.py:86
  59.2 0.1 fusion.19
  59.2 1.3 %collective-permute-start = (f32[16,1,8192]{2,0,1:T(8,128)S(1)}, f32[16,1,8192]{2,0,1:T(8,128)S(1)}, u32[]{:S(2)}, u32[]{:S(2)}) collective-permute-start(f32[16,1,8192]{2,0,1:T(8,128)S(1)} %get-tuple-element.8), channel_id=1, source_target_pairs={{4,0},{8,4},{12,8},{16,12},{20,16},{24,20},{28,24},{5,1},{9,5},{13... | collective-permute-start | bytes 1572872 | tf_op jit(solution)/shard_map/ppermute | solution.py:22
  60.5 4.8 %collective-permute-start.2 = (f32[16,1,8192]{2,0,1:T(8,128)S(1)}, f32[16,1,8192]{2,0,1:T(8,128)S(1)}, u32[]{:S(2)}, u32[]{:S(2)}) collective-permute-start(f32[16,1,8192]{2,0,1:T(8,128)S(1)} %get-tuple-element.9), channel_id=1, source_target_pairs={{0,4},{4,8},{8,12},{12,16},{16,20},{20,24},{24,28},{1,5},{5,9},{9,... | collective-permute-start | bytes 1572872 | tf_op jit(solution)/shard_map/ppermute | solution.py:21
  65.4 1.5 %fusion.18 = (f32[16,8,8191]{2,0,1:T(8,128)S(1)}, f32[16,8,8191]{2,0,1:T(8,128)S(1)}) fusion(f32[16,8,8192]{2,0,1:T(8,128)S(1)} %bitcast.28), kind=kLoop, calls=%fused_computation.47 | loop fusion | bytes 16775168 | tf_op jit(solution)/shard_map/slice | solution.py:28
  66.8 8.2 %collective-permute-done = f32[16,1,8192]{2,0,1:T(8,128)S(1)} collective-permute-done((f32[16,1,8192]{2,0,1:T(8,128)S(1)}, f32[16,1,8192]{2,0,1:T(8,128)S(1)}, u32[]{:S(2)}, u32[]{:S(2)}) %collective-permute-start) | collective-permute-done | bytes 524320 | tf_op jit(solution)/shard_map/ppermute | solution.py:22
  75.0 11.4 %collective-permute-done.2 = f32[16,1,8192]{2,0,1:T(8,128)S(1)} collective-permute-done((f32[16,1,8192]{2,0,1:T(8,128)S(1)}, f32[16,1,8192]{2,0,1:T(8,128)S(1)}, u32[]{:S(2)}, u32[]{:S(2)}) %collective-permute-start.2) | collective-permute-done | bytes 524320 | tf_op jit(solution)/shard_map/ppermute | solution.py:21
  86.4 7.7 %multiply_reduce_fusion = (f32[16]{0:T(128)S(1)}, f32[16,8,8192]{2,0,1:T(8,128)}) fusion(s32[16]{0:T(128)S(1)} %dynamic_slice.3, s32[8,8192]{1,0:T(8,128)S(1)} %iota_add_fusion, f32[16,8,8192]{2,0,1:T(8,128)S(1)} %bitcast.29, f32[16,1,8192]{2,0,1:T(8,128)S(1)} %collective-permute-done.2, f32[8,8192]{1,0:T(8,128)S(1)} %get-tuple-element.22, ...), kind=kLoop, calls=%fused_computation.23 | loop fusion | flops 35651568 | bytes 19922048 | tf_op jit(solution)/shard_map/reduce_sum | solution.py:92
  94.1 19.8 %psum.7 = f32[16]{0:T(128)S(1)} all-reduce(f32[16]{0:T(128)S(1)} %get-tuple-element.4), channel_id=1, replica_groups=mesh['vtx'=8,'src'=4] {'vtx'}, use_global_device_ids=true, to_apply=%region_1.2 | all-reduce | flops 16 | bytes 128 | tf_op jit(solution)/shard_map/psum | solution.py:92
  114.0 0.0 copy-start.1
  114.0 2.7 %broadcast_divide_fusion = f32[16,8,8192]{2,0,1:T(8,128)S(1)} fusion(f32[16,8,8192]{2,0,1:T(8,128)} %get-tuple-element.5, f32[16]{0:T(128)S(1)} %add_sqrt_fusion), kind=kLoop, calls=%fused_computation.24 | loop fusion | flops 1048576 | bytes 8388672 | tf_op jit(solution)/shard_map/div | solution.py:94
  116.7 0.0 copy-done.1
  116.7 4.4 %copy.7 = f32[16,8,8192]{2,1,0:T(8,128)} copy(f32[16,8,8192]{2,0,1:T(8,128)S(1)} %broadcast_divide_fusion) | data formatting | bytes 8388608
  (8 shorter events, 0.1 us)
Async XLA Ops:
  0.6 5.0 %copy-start = (f32[4,8,8192]{2,1,0:T(8,128)S(1)}, f32[4,8,8192]{2,1,0:T(8,128)}, u32[]{:S(2)}) copy-start(f32[4,8,8192]{2,1,0:T(8,128)} %param.4) | copy-start | bytes 3145732
  0.6 53.9 %all-to-all-start = ((f32[64,2,8192]{2,1,0:T(2,128)}), f32[64,2,8192]{2,1,0:T(2,128)}, u32[]{:S(2)}, u32[]{:S(2)}) async-start(f32[64,2,8192]{2,1,0:T(2,128)} %param.3), calls=%async_computation | async-start | bytes 8388608 | tf_op jit(solution)/shard_map/all_to_all | solution.py:86
  5.6 5.5 %copy-start.2 = (s32[64]{0:T(128)S(1)}, s32[64]{0:T(128)}, u32[]{:S(2)}) copy-start(s32[64]{0:T(128)} %param.5) | copy-start | bytes 772
  5.9 6.8 %collective-permute-start.1 = (f32[2,1,8192]{2,1,0:T(1,128)S(1)}, f32[2,1,8192]{2,1,0:T(1,128)S(1)}, u32[]{:S(2)}, u32[]{:S(2)}) collective-permute-start(f32[2,1,8192]{2,1,0:T(1,128)S(1)} %pad_maximum_fusion.1), channel_id=1, source_target_pairs={{0,4},{4,8},{8,12},{12,16},{16,20},{20,24},{24,28},{1,5},{5,9},{9,... | collective-permute-start | bytes 196616 | tf_op jit(solution)/shard_map/ppermute | solution.py:11
  59.2 15.8 %collective-permute-start = (f32[16,1,8192]{2,0,1:T(8,128)S(1)}, f32[16,1,8192]{2,0,1:T(8,128)S(1)}, u32[]{:S(2)}, u32[]{:S(2)}) collective-permute-start(f32[16,1,8192]{2,0,1:T(8,128)S(1)} %get-tuple-element.8), channel_id=1, source_target_pairs={{4,0},{8,4},{12,8},{16,12},{20,16},{24,20},{28,24},{5,1},{9,5},{13... | collective-permute-start | bytes 1572872 | tf_op jit(solution)/shard_map/ppermute | solution.py:22
  60.5 25.9 %collective-permute-start.2 = (f32[16,1,8192]{2,0,1:T(8,128)S(1)}, f32[16,1,8192]{2,0,1:T(8,128)S(1)}, u32[]{:S(2)}, u32[]{:S(2)}) collective-permute-start(f32[16,1,8192]{2,0,1:T(8,128)S(1)} %get-tuple-element.9), channel_id=1, source_target_pairs={{0,4},{4,8},{8,12},{12,16},{16,20},{20,24},{24,28},{1,5},{5,9},{9,... | collective-permute-start | bytes 1572872 | tf_op jit(solution)/shard_map/ppermute | solution.py:21
  114.0 2.7 %copy-start.1 = (f32[16]{0:T(128)}, f32[16]{0:T(128)S(1)}, u32[]{:S(2)}) copy-start(f32[16]{0:T(128)S(1)} %add_sqrt_fusion) | copy-start | bytes 196
where the time goes:
time: 122 us; the launch traced here: 121 us
  waiting for transfers between devices  62.6 us (51%)
  blocking collectives  19.8 us (16%)
  starting transfers between devices  15.9 us (13%)
  other arithmetic  11.1 us (9%)
  local copies, waits for them, and re-layouts  10.9 us (9%)
    all_to_all x1, waiting for transfers between devices, on_device(): tile = lax.all_to_all(heat, 'src', split_axis=0, concat_axis=1, tiled=True)  41.6 us
    psum x1, blocking collectives, on_device(): total = lax.psum(jnp.sum(defect * defect, axis=(1, 2)), 'vtx')  19.8 us
    ppermute x1, waiting for transfers between devices, extended(): before = lax.ppermute(last, axis, up)  11.4 us
    ppermute x1, waiting for transfers between devices, extended(): after = lax.ppermute(first, axis, down)  8.19 us
    reduce_sum x1, other arithmetic, on_device(): total = lax.psum(jnp.sum(defect * defect, axis=(1, 2)), 'vtx')  7.71 us
    all_to_all x1, starting transfers between devices, on_device(): tile = lax.all_to_all(heat, 'src', split_axis=0, concat_axis=1, tiled=True)  4.97 us
    ppermute x1, starting transfers between devices, from_behind(): return lax.ppermute(value, axis, pairs)  4.87 us
    ppermute x1, starting transfers between devices, extended(): before = lax.ppermute(last, axis, up)  4.81 us
  transfers between devices with their start and end apart: 4, of which 4 were waited for; matrix products, arithmetic and copies ran while one was open for 2% of the time, Pallas kernels for 0%

commit v1 on v0

--- a/solution.py
+++ b/solution.py
@@ -89,7 +89,7 @@
     defect = stencil_defect(
         padded, mass, east, north_ext, diag_ext, block_start, sources, amplitude
     )
-    total = lax.psum(jnp.sum(defect * defect, axis=(1, 2)), "vtx")
+    total = jnp.sum(lax.all_gather(jnp.sum(defect * defect, axis=(1, 2)), "vtx"), axis=0)
     norms = jnp.sqrt(total / (total_rows * width) + 1e-06)
     return (defect / norms[:, None, None], norms)
 

time: 122 us -> 127 us (1.041)
  waiting for transfers between devices: 62.6 us -> 65.3 us
    psum x1 -> x0, blocking collectives: 19.8 us -> none  [on_device(): total = lax.psum(jnp.sum(defect * defect, axis=(1, 2)), 'vtx')]
    unnamed x0 -> x1, blocking collectives: none -> 19.8 us
    all_to_all x1, waiting for transfers between devices: 41.6 us -> 46.2 us  [on_device(): tile = lax.all_to_all(heat, 'src', split_axis=0, concat_axis=1, tiled=True)]
    ppermute x1, waiting for transfers between devices: 1.44 us -> 0.01 us  [from_behind(): return lax.ppermute(value, axis, pairs)]
    unnamed x7 -> x12, local copies, waits for them, and re-layouts: 4.46 us -> 5.29 us
    reduce_sum x1 -> x2, other arithmetic: 7.71 us -> 7.73 us  [the longest x1 7.71 us: on_device(): jnp.sum(defect * defect, axis=(1, 2))]
  transfers between devices with their start and end apart: 4 -> 4, of which waited for: 4 -> 3; matrix products, arithmetic and copies ran while one was open for 2% -> 2% of each run, Pallas kernels for 0% -> 0%
where the time goes in v1:
time: 127 us; the launch traced here: 126 us
  waiting for transfers between devices  65.3 us (51%)
  blocking collectives  19.8 us (16%)
  starting transfers between devices  15.7 us (12%)
  other arithmetic  12.1 us (10%)
  local copies, waits for them, and re-layouts  11.8 us (9%)
  between operations  1.51 us (1%)
    all_to_all x1, waiting for transfers between devices, on_device(): tile = lax.all_to_all(heat, 'src', split_axis=0, concat_axis=1, tiled=True)  46.2 us
    unnamed x1, blocking collectives  19.8 us
    ppermute x1, waiting for transfers between devices, extended(): before = lax.ppermute(last, axis, up)  11.2 us
    ppermute x1, waiting for transfers between devices, extended(): after = lax.ppermute(first, axis, down)  7.91 us
    reduce_sum x1, other arithmetic, on_device(): jnp.sum(defect * defect, axis=(1, 2))  7.71 us
    unnamed x12, local copies, waits for them, and re-layouts  5.29 us
    ppermute x1, starting transfers between devices, from_behind(): return lax.ppermute(value, axis, pairs)  5.01 us
    all_to_all x1, starting transfers between devices, on_device(): tile = lax.all_to_all(heat, 'src', split_axis=0, concat_axis=1, tiled=True)  4.85 us
  transfers between devices with their start and end apart: 4, of which 3 were waited for; matrix products, arithmetic and copies ran while one was open for 2% of the time, Pallas kernels for 0%

profile of v1, /device:TPU:0, one launch (start us, length us, event | category | flops | bytes accessed | tf_op | source)
XLA Modules:
  0.0 126.3 jit_solution(1844966854184624672)
XLA Ops:
  0.7 1.1 bitcast_select_fusion.1
  1.9 0.1 pad_maximum_fusion.1
  2.0 0.0 copy-start
  2.0 0.0 copy-start.2
  2.0 0.0 copy-start.3
  2.0 5.0 %collective-permute-start.1 = (f32[2,1,8192]{2,1,0:T(1,128)S(1)}, f32[2,1,8192]{2,1,0:T(1,128)S(1)}, u32[]{:S(2)}, u32[]{:S(2)}) collective-permute-start(f32[2,1,8192]{2,1,0:T(1,128)S(1)} %pad_maximum_fusion.1), channel_id=1, source_target_pairs={{0,4},{4,8},{8,12},{12,16},{16,20},{20,24},{24,28},{1,5},{5,9},{9,... | collective-permute-start | bytes 196616 | tf_op jit(solution)/shard_map/ppermute | solution.py:11
  7.0 4.8 %all-to-all-start = ((f32[64,2,8192]{2,1,0:T(2,128)}), f32[64,2,8192]{2,1,0:T(2,128)}, u32[]{:S(2)}, u32[]{:S(2)}) async-start(f32[64,2,8192]{2,1,0:T(2,128)} %param.3), calls=%async_computation | async-start | bytes 8388608 | tf_op jit(solution)/shard_map/all_to_all | solution.py:86
  11.9 0.0 copy-done
  11.9 0.1 slice_bitcast_fusion
  12.1 0.1 iota_add_fusion
  12.2 0.1 concatenate.32
  12.3 0.0 copy-done.2
  12.3 0.1 dynamic_slice.3
  12.4 0.0 copy-done.3
  12.4 0.6 dynamic-slice
  13.6 0.0 collective-permute-done.1
  13.6 0.2 select_maximum_fusion.2
  13.9 46.2 %all-to-all-done = f32[64,2,8192]{2,1,0:T(2,128)} async-done(((f32[64,2,8192]{2,1,0:T(2,128)}), f32[64,2,8192]{2,1,0:T(2,128)}, u32[]{:S(2)}, u32[]{:S(2)}) %all-to-all-start) | async-done | bytes 4194336 | tf_op jit(solution)/shard_map/all_to_all | solution.py:86
  60.1 4.6 %copy.6 = f32[4,16,2,8192]{3,1,2,0:T(8,128)S(1)} copy(f32[4,16,2,8192]{3,2,1,0:T(2,128)} %bitcast.1) | data formatting | bytes 8388608 | tf_op jit(solution)/shard_map/all_to_all | solution.py:86
  64.7 0.1 fusion.19
  64.8 1.3 %collective-permute-start = (f32[16,1,8192]{2,0,1:T(8,128)S(1)}, f32[16,1,8192]{2,0,1:T(8,128)S(1)}, u32[]{:S(2)}, u32[]{:S(2)}) collective-permute-start(f32[16,1,8192]{2,0,1:T(8,128)S(1)} %get-tuple-element.8), channel_id=1, source_target_pairs={{4,0},{8,4},{12,8},{16,12},{20,16},{24,20},{28,24},{5,1},{9,5},{13... | collective-permute-start | bytes 1572872 | tf_op jit(solution)/shard_map/ppermute | solution.py:22
  66.1 4.6 %collective-permute-start.2 = (f32[16,1,8192]{2,0,1:T(8,128)S(1)}, f32[16,1,8192]{2,0,1:T(8,128)S(1)}, u32[]{:S(2)}, u32[]{:S(2)}) collective-permute-start(f32[16,1,8192]{2,0,1:T(8,128)S(1)} %get-tuple-element.9), channel_id=1, source_target_pairs={{0,4},{4,8},{8,12},{12,16},{16,20},{20,24},{24,28},{1,5},{5,9},{9,... | collective-permute-start | bytes 1572872 | tf_op jit(solution)/shard_map/ppermute | solution.py:21
  70.7 1.5 %fusion.18 = (f32[16,8,8191]{2,0,1:T(8,128)S(1)}, f32[16,8,8191]{2,0,1:T(8,128)S(1)}) fusion(f32[16,8,8192]{2,0,1:T(8,128)S(1)} %bitcast.29), kind=kLoop, calls=%fused_computation.47 | loop fusion | bytes 16775168 | tf_op jit(solution)/shard_map/slice | solution.py:28
  72.1 7.9 %collective-permute-done = f32[16,1,8192]{2,0,1:T(8,128)S(1)} collective-permute-done((f32[16,1,8192]{2,0,1:T(8,128)S(1)}, f32[16,1,8192]{2,0,1:T(8,128)S(1)}, u32[]{:S(2)}, u32[]{:S(2)}) %collective-permute-start) | collective-permute-done | bytes 524320 | tf_op jit(solution)/shard_map/ppermute | solution.py:22
  80.0 11.2 %collective-permute-done.2 = f32[16,1,8192]{2,0,1:T(8,128)S(1)} collective-permute-done((f32[16,1,8192]{2,0,1:T(8,128)S(1)}, f32[16,1,8192]{2,0,1:T(8,128)S(1)}, u32[]{:S(2)}, u32[]{:S(2)}) %collective-permute-start.2) | collective-permute-done | bytes 524320 | tf_op jit(solution)/shard_map/ppermute | solution.py:21
  91.2 7.7 %multiply_reduce_fusion = (f32[16]{0:T(128)S(1)}, f32[16,8,8192]{2,0,1:T(8,128)}) fusion(s32[16]{0:T(128)S(1)} %dynamic_slice.3, s32[8,8192]{1,0:T(8,128)S(1)} %iota_add_fusion, f32[16,8,8192]{2,0,1:T(8,128)S(1)} %bitcast.30, f32[16,1,8192]{2,0,1:T(8,128)S(1)} %collective-permute-done.2, f32[8,8192]{1,0:T(8,128)S(1)} %get-tuple-element.22, ...), kind=kLoop, calls=%fused_computation.23 | loop fusion | flops 35651568 | bytes 19922048 | tf_op jit(solution)/shard_map/reduce_sum | solution.py:92
  98.9 0.2 dynamic-update-slice
  99.2 19.8 %all-reduce.6 = f32[128]{0:T(128)S(1)} all-reduce(f32[128]{0:T(128)S(1)} %dynamic-update-slice), channel_id=2, replica_groups=mesh['vtx'=8,'src'=4] {'vtx'}, use_global_device_ids=true, to_apply=%add.6 | all-reduce | flops 128 | bytes 1024
  119.0 0.1 reshape.77
  119.1 2.7 %broadcast_divide_fusion = f32[16,8,8192]{2,0,1:T(8,128)S(1)} fusion(f32[16,8,8192]{2,0,1:T(8,128)} %get-tuple-element.5, f32[16]{0:T(128)S(1)} %add_sqrt_fusion), kind=kLoop, calls=%fused_computation.24 | loop fusion | flops 1048576 | bytes 8388672 | tf_op jit(solution)/shard_map/div | solution.py:94
  121.9 0.0 copy-done.1
  121.9 4.4 %copy.7 = f32[16,8,8192]{2,1,0:T(8,128)} copy(f32[16,8,8192]{2,0,1:T(8,128)S(1)} %broadcast_divide_fusion) | data formatting | bytes 8388608
  (11 shorter events, 0.2 us)
Async XLA Ops:
  2.0 9.9 %copy-start = (f32[4,8,8192]{2,1,0:T(8,128)S(1)}, f32[4,8,8192]{2,1,0:T(8,128)}, u32[]{:S(2)}) copy-start(f32[4,8,8192]{2,1,0:T(8,128)} %param.4) | copy-start | bytes 3145732
  2.0 10.3 %copy-start.2 = (s32[64]{0:T(128)S(1)}, s32[64]{0:T(128)}, u32[]{:S(2)}) copy-start(s32[64]{0:T(128)} %param.5) | copy-start | bytes 772
  2.0 10.4 %copy-start.3 = (u32[32]{0:T(128)S(1)}, u32[32]{0:T(128)}, u32[]{:S(2)}) copy-start(u32[32]{0:T(128)} %constant.50) | copy-start | bytes 388
  2.0 11.6 %collective-permute-start.1 = (f32[2,1,8192]{2,1,0:T(1,128)S(1)}, f32[2,1,8192]{2,1,0:T(1,128)S(1)}, u32[]{:S(2)}, u32[]{:S(2)}) collective-permute-start(f32[2,1,8192]{2,1,0:T(1,128)S(1)} %pad_maximum_fusion.1), channel_id=1, source_target_pairs={{0,4},{4,8},{8,12},{12,16},{16,20},{20,24},{24,28},{1,5},{5,9},{9,... | collective-permute-start | bytes 196616 | tf_op jit(solution)/shard_map/ppermute | solution.py:11
  7.0 53.1 %all-to-all-start = ((f32[64,2,8192]{2,1,0:T(2,128)}), f32[64,2,8192]{2,1,0:T(2,128)}, u32[]{:S(2)}, u32[]{:S(2)}) async-start(f32[64,2,8192]{2,1,0:T(2,128)} %param.3), calls=%async_computation | async-start | bytes 8388608 | tf_op jit(solution)/shard_map/all_to_all | solution.py:86
  64.8 15.3 %collective-permute-start = (f32[16,1,8192]{2,0,1:T(8,128)S(1)}, f32[16,1,8192]{2,0,1:T(8,128)S(1)}, u32[]{:S(2)}, u32[]{:S(2)}) collective-permute-start(f32[16,1,8192]{2,0,1:T(8,128)S(1)} %get-tuple-element.8), channel_id=1, source_target_pairs={{4,0},{8,4},{12,8},{16,12},{20,16},{24,20},{28,24},{5,1},{9,5},{13... | collective-permute-start | bytes 1572872 | tf_op jit(solution)/shard_map/ppermute | solution.py:22
  66.1 25.2 %collective-permute-start.2 = (f32[16,1,8192]{2,0,1:T(8,128)S(1)}, f32[16,1,8192]{2,0,1:T(8,128)S(1)}, u32[]{:S(2)}, u32[]{:S(2)}) collective-permute-start(f32[16,1,8192]{2,0,1:T(8,128)S(1)} %get-tuple-element.9), channel_id=1, source_target_pairs={{0,4},{4,8},{8,12},{12,16},{16,20},{20,24},{24,28},{1,5},{5,9},{9,... | collective-permute-start | bytes 1572872 | tf_op jit(solution)/shard_map/ppermute | solution.py:21
  119.1 2.7 %copy-start.1 = (f32[16]{0:T(128)}, f32[16]{0:T(128)S(1)}, u32[]{:S(2)}) copy-start(f32[16]{0:T(128)S(1)} %add_sqrt_fusion) | copy-start | bytes 196
